TPU v7x, 32 devices: a whole 2x2x4 slice. The times are simulated.
32 devices in a mesh: row: 16 (over z, y, core), col: 2 (over x).
Axes of the slice: x: 2, y: 2, z: 4, core: 2. Of those that a mesh axis runs over, the one named last changes fastest.
Arguments:
- kernel: float32 [5120, 65536], P('row', 'col'), may hold values from -0.0234375 to 0.0234375
- slip: float32 [512, 65536], P('row', 'col'), may hold values from -6 to 6
- segment: int32 [5120], P(('row', 'col')), may hold values from 0 to 15
- prestress: float32 [5120, 512], P(('row', 'col')), may hold values from -4 to 4
- state: float32 [5120, 512], P(('row', 'col')), may hold values from 0.5 to 2
- normal_stress: float32 [5120], P(('row', 'col')), may hold values from 2 to 8
- a_table: float32 [16], replicated, may hold values from 0.5 to 1
- b_table: float32 [16], replicated, may hold values from 0.5 to 1
Outputs:
- new_rate: float32 [5120, 512], P(('row', 'col'))
- new_state: float32 [5120, 512], P(('row', 'col'))
All inputs are finite; a program needn't handle non-finite values.
Results may differ from a plain program's by a relative error of at most 0.00016.
Values sent between devices are 32-bit elements; how exact they have to be, the bound alone decides.
A program may use at most 192 MiB of HBM per device.

v0:
```python
import functools

import jax
import jax.numpy as jnp
from jax import lax
from jax.experimental import pallas as pl
from jax.experimental.pallas import tpu as pltpu
from jax.sharding import PartitionSpec as P

CHUNKS = 16
MESH = pl.DeviceIdType.MESH


def split(value):
    high = value.astype(jnp.bfloat16)
    return high, (value - high.astype(jnp.float32)).astype(jnp.bfloat16)


def times(left, right):
    return lax.dot_general(
        left, right, (((1,), (1,)), ((), ())), preferred_element_type=jnp.float32
    )


def gather_product(
    rows, kernel_ref, slip_ref, total, held, slip_in, kernel_in,
    ring_send, ring_recv, pair_send, pair_recv, own_send, own_recv, slip_sem, kernel_sem,
):
    members = slip_ref.shape[0]
    width = slip_ref.shape[1] // CHUNKS
    chips = rows // 2
    rounds = chips - 1
    pairs = CHUNKS // 2
    me = lax.axis_index("row")
    core = lax.rem(me, 2)
    other = me + 1 - 2 * core
    chip = me // 2
    odd = chip % 2
    place = (1 - odd) * (chip // 2) + odd * (chips - 1 - chip // 2)

    def row_at(spot, which):
        spot = (spot + chips) % chips
        back = spot // (chips // 2)
        return ((1 - back) * 2 * spot + back * (2 * (chips - 1 - spot) + 1)) * 2 + which

    def block(ref, row, chunk):
        return ref.at[
            pl.ds(pl.multiple_of(row * members, members), members),
            pl.ds(pl.multiple_of(chunk * width, width), width),
        ]

    def own(chunk):
        return slip_ref.at[:, pl.ds(pl.multiple_of(chunk * width, width), width)]

    def chunk_of(pair, way, step):
        return 2 * pair + (step + way) % 2

    def origin(way, hops):
        return place - hops if way == 0 else place + hops

    def ring(pair, way, step):
        chunk = chunk_of(pair, way, step)
        hops = step // 2
        row = row_at(origin(way, hops), core)
        return pltpu.make_async_remote_copy(
            src_ref=own(chunk) if hops == 0 else block(held, row, chunk),
            dst_ref=block(held, row, chunk),
            send_sem=ring_send.at[way, step],
            recv_sem=ring_recv.at[pair % 2, way, step],
            device_id={"row": row_at(place + 1 if way == 0 else place - 1, core)},
            device_id_type=MESH,
        )

    def across(pair, way, step):
        chunk = chunk_of(pair, way, step)
        piece = block(held, row_at(origin(way, step // 2 + 1), core), chunk)
        return pltpu.make_async_remote_copy(
            src_ref=piece,
            dst_ref=piece,
            send_sem=pair_send.at[way, step],
            recv_sem=pair_recv.at[pair % 3, way, step],
            device_id={"row": other},
            device_id_type=MESH,
        )

    def across_own(pair, side):
        chunk = 2 * pair + side
        return pltpu.make_async_remote_copy(
            src_ref=own(chunk),
            dst_ref=block(held, me, chunk),
            send_sem=own_send.at[side],
            recv_sem=own_recv.at[pair % 3, side],
            device_id={"row": other},
            device_id_type=MESH,
        )

    def kernel_load(chunk, side):
        return pltpu.make_async_copy(
            kernel_ref.at[:, pl.ds(pl.multiple_of(chunk * width, width), width)],
            kernel_in.at[side],
            kernel_sem.at[side],
        )

    def slip_start(chunk, side):
        def place_in(row):
            return slip_in.at[side, pl.ds(pl.multiple_of(row * members, members), members)]

        pltpu.make_async_copy(own(chunk), place_in(me), slip_sem.at[side]).start()

        def one(at, carry):
            row = (me + at) % rows
            pltpu.make_async_copy(
                block(held, row, chunk), place_in(row), slip_sem.at[side]
            ).start()
            return carry

        lax.fori_loop(1, rows, one, 0)

    def slip_wait(chunk, side):
        pltpu.make_async_copy(
            held.at[:, pl.ds(pl.multiple_of(chunk * width, width), width)],
            slip_in.at[side],
            slip_sem.at[side],
        ).wait()

    depth = min(width, 512)

    def product(side):
        def one(at, carry):
            columns = pl.ds(pl.multiple_of(at * depth, depth), depth)
            k_high, k_low = split(kernel_in[side, :, columns])
            s_high, s_low = split(slip_in[side, :, columns])
            total[...] += times(k_high, s_high) + (times(k_high, s_low) + times(k_low, s_high))
            return carry

        lax.fori_loop(0, width // depth, one, 0)

    total[...] = jnp.zeros_like(total)

    def arrival(pair, way, step):
        ring(pair, way, step).wait_recv()

    def pass_across(pair, way, step):
        @pl.when(pair > 0)
        def _():
            across(pair, way, step).wait_send()

        across(pair, way, step).start()

    def travel(pair, carry):
        sending = pair < pairs
        draining = pair > 0
        for step in range(rounds):

            @pl.when(sending)
            def _():
                for way in range(2):
                    if step >= 2:
                        arrival(pair, way, step - 2)

                    @pl.when(draining)
                    def _():
                        ring(pair, way, step).wait_send()

                    ring(pair, way, step).start()
                if step < 2:

                    @pl.when(draining)
                    def _():
                        across_own(pair, step).wait_send()

                    across_own(pair, step).start()
                else:
                    for way in range(2):
                        pass_across(pair, way, step - 2)

            @pl.when(draining)
            def _():
                if step < 2:
                    for way in range(2):
                        arrival(pair - 1, way, rounds - 2 + step)
                        pass_across(pair - 1, way, rounds - 2 + step)
                if step == 0:
                    for side in range(2):
                        kernel_load(2 * pair - 2 + side, side).start()
                if step == 2:
                    for side in range(2):
                        across_own(pair - 1, side).wait_recv()
                    for way in range(2):
                        for back in range(rounds):
                            across(pair - 1, way, back).wait_recv()
                    for side in range(2):
                        slip_start(2 * pair - 2 + side, side)
                if step in (3, 5):
                    side = (step - 3) // 2
                    kernel_load(2 * pair - 2 + side, side).wait()
                    slip_wait(2 * pair - 2 + side, side)
                    product(side)

        return carry

    lax.fori_loop(0, pairs + 1, travel, 0)
    last = pairs - 1
    for way in range(2):
        for step in range(rounds):
            ring(last, way, step).wait_send()
            across(last, way, step).wait_send()
    for side in range(2):
        across_own(last, side).wait_send()


def traction_partial(rows, kernel, slip):
    targets, columns = kernel.shape
    members = slip.shape[0] * rows
    width = columns // CHUNKS
    rounds = rows // 2 - 1
    dma = pltpu.SemaphoreType.DMA
    flops = 6 * targets * members * columns
    return pl.pallas_call(
        functools.partial(gather_product, rows),
        out_shape=(
            jax.ShapeDtypeStruct((targets, members), jnp.float32),
            jax.ShapeDtypeStruct((members, columns), jnp.float32),
        ),
        in_specs=[pl.BlockSpec(memory_space=pl.ANY)] * 2,
        out_specs=(pl.BlockSpec(memory_space=pltpu.VMEM), pl.BlockSpec(memory_space=pl.ANY)),
        scratch_shapes=[
            pltpu.VMEM((2, members, width), jnp.float32),
            pltpu.VMEM((2, targets, width), jnp.float32),
            dma((2, rounds)),
            dma((2, 2, rounds)),
            dma((2, rounds)),
            dma((3, 2, rounds)),
            dma((2,)),
            dma((3, 2)),
            dma((2,)),
            dma((2,)),
        ],
        compiler_params=pltpu.CompilerParams(
            has_side_effects=True, vmem_limit_bytes=48 * 1024 * 1024
        ),
        cost_estimate=pl.CostEstimate(
            flops=flops, bytes_accessed=4 * members * columns * 4, transcendentals=0
        ),
    )(kernel, slip)[0]


def add_over_columns(partial_value, columns):
    if columns != 2:
        return lax.psum_scatter(partial_value, "col", scatter_dimension=0, tiled=True)
    half = partial_value.shape[0] // 2
    me = lax.axis_index("col")
    mine = lax.dynamic_slice_in_dim(partial_value, me * half, half, 0)
    theirs = lax.dynamic_slice_in_dim(partial_value, (1 - me) * half, half, 0)
    return mine + lax.ppermute(theirs, "col", [(0, 1), (1, 0)])


def friction(traction, segment, prestress, state, normal_stress, a_table, b_table):
    onehot = (segment[:, None] == jnp.arange(a_table.shape[0], dtype=jnp.int32)[None, :]).astype(
        jnp.float32
    )
    a_rows = jnp.dot(onehot, a_table, precision=lax.Precision.HIGHEST)
    b_rows = jnp.dot(onehot, b_table, precision=lax.Precision.HIGHEST)
    stress = prestress + traction
    new_rate = jnp.exp(-(b_rows / a_rows)[:, None] * jnp.log(state)) * jnp.sinh(
        stress / (a_rows * normal_stress)[:, None]
    )
    new_state = state + 0.1 * (1.0 - new_rate * state)
    return (new_rate, new_state)


def per_device(rows, columns, kernel, slip, segment, prestress, state, normal_stress, a_table, b_table):
    traction = add_over_columns(traction_partial(rows, kernel, slip), columns)
    return friction(traction, segment, prestress, state, normal_stress, a_table, b_table)


def solution(mesh):
    placed = (
        P("row", "col"),
        P("row", "col"),
        P(("row", "col")),
        P(("row", "col"), None),
        P(("row", "col"), None),
        P(("row", "col")),
        P(),
        P(),
    )
    return jax.shard_map(
        functools.partial(per_device, mesh.shape["row"], mesh.shape["col"]),
        mesh=mesh,
        in_specs=placed,
        out_specs=(P(("row", "col"), None), P(("row", "col"), None)),
        check_vma=False,
    )
```

profile of v0, /device:TPU:0, one launch (start us, length us, event | category | flops | bytes accessed | tf_op | source)
XLA Modules:
  0.0 349.8 jit_solution(4532020639833581238)
XLA Ops:
  0.6 0.0 copy-start
  0.7 0.0 copy-start.1
  0.7 2.2 copy-done.1
  2.8 0.0 copy-start.5
  2.8 0.0 copy-start.6
  2.8 0.0 copy-start.4
  2.8 0.0 copy-start.2
  2.9 0.0 copy-start.3
  2.9 334.9 %shard_map.95 = (f32[320,512]{1,0:T(8,128)S(1)}, f32[512,32768]{1,0:T(8,128)}) custom-call(f32[320,32768]{1,0:T(8,128)} %kernel_ref.1, f32[32,32768]{1,0:T(8,128)S(1)} %copy-done.1), custom_call_target="tpu_custom_call" | custom-call | flops 32212254720 | bytes 268435456 | tf_op jit(solution)/shard_map/pallas_call | solution.py:219
  337.8 1.5 collective-permute-start
  339.4 0.0 copy-done
  339.4 0.0 copy-done.5
  339.4 0.2 fusion.4
  339.6 0.0 copy-done.6
  339.6 0.3 fusion.3
  339.8 0.0 copy-done.4
  339.8 0.1 divide_negate_fusion
  339.9 8.5 %collective-permute-done = f32[160,512]{1,0:T(8,128)S(1)} collective-permute-done((f32[160,512]{1,0:T(8,128)S(1)}, f32[160,512]{1,0:T(8,128)S(1)}, u32[]{:S(2)}, u32[]{:S(2)}) %collective-permute-start) | collective-permute-done | bytes 327712 | tf_op jit(solution)/shard_map/ppermute | solution.py:255
  348.5 0.0 copy-done.2
  348.5 0.0 copy-done.3
  348.5 1.3 multiply_add_fusion
  (1 shorter events, 0.0 us)
Async XLA Ops:
  0.6 338.7 %copy-start = (f32[16]{0:T(128)S(1)}, f32[16]{0:T(128)}, u32[]{:S(2)}) copy-start(f32[16]{0:T(128)} %param.15) | copy-start | bytes 196
  0.7 2.2 copy-start.1
  2.8 336.5 %copy-start.5 = (s32[160]{0:T(256)S(1)}, s32[160]{0:T(256)}, u32[]{:S(2)}) copy-start(s32[160]{0:T(256)} %param.10) | copy-start | bytes 1924
  2.8 336.7 %copy-start.6 = (f32[16]{0:T(128)S(1)}, f32[16]{0:T(128)}, u32[]{:S(2)}) copy-start(f32[16]{0:T(128)} %param.14) | copy-start | bytes 196
  2.8 337.0 %copy-start.4 = (f32[160]{0:T(256)S(1)}, f32[160]{0:T(256)}, u32[]{:S(2)}) copy-start(f32[160]{0:T(256)} %param.13) | copy-start | bytes 1924
  2.8 345.6 %copy-start.2 = (f32[160,512]{1,0:T(8,128)S(1)}, f32[160,512]{1,0:T(8,128)}, u32[]{:S(2)}) copy-start(f32[160,512]{1,0:T(8,128)} %param.12) | copy-start | bytes 983044
  2.9 345.6 %copy-start.3 = (f32[160,512]{1,0:T(8,128)S(1)}, f32[160,512]{1,0:T(8,128)}, u32[]{:S(2)}) copy-start(f32[160,512]{1,0:T(8,128)} %param.11) | copy-start | bytes 983044
  337.8 10.6 %collective-permute-start = (f32[160,512]{1,0:T(8,128)S(1)}, f32[160,512]{1,0:T(8,128)S(1)}, u32[]{:S(2)}, u32[]{:S(2)}) collective-permute-start(f32[160,512]{1,0:T(8,128)S(1)} %constant_dynamic-slice_fusion), channel_id=1, source_target_pairs={{0,1},{1,0},{2,3},{3,2},{4,5},{5,4},{6,7},{7,6},{8,9},{9,8},{10,11... | collective-permute-start | bytes 983048 | tf_op jit(solution)/shard_map/ppermute | solution.py:255
where the time goes:
time: 350 us
  Pallas kernels  335 us (96%)
  waiting for transfers between devices  8.54 us (2%)
    pallas_call x1, Pallas kernels, traction_partial(): pl.pallas_call(functools.partial(gather_product, rows), out_shape=(jax.Sh...  335 us
    ppermute x1, waiting for transfers between devices, add_over_columns(): return mine + lax.ppermute(theirs, 'col', [(0, 1), (1, 0)])  8.54 us
  transfers between devices with their start and end apart: 1, of which 1 were waited for; matrix products, arithmetic and copies ran while one was open for 0% of the time, Pallas kernels for 0%

commit v1 on v0

--- a/solution.py
+++ b/solution.py
@@ -245,6 +245,338 @@
     )(kernel, slip)[0]
 
 
+BESIDE, PARTNER, ACROSS = 1, 2, 6
+SLOTS = 32
+LAG = 2
+KERNEL_LAG = 4
+LANES = 128
+MIDDLE = {
+    0: (0, (ACROSS, BESIDE, PARTNER)),
+    2: (1, (ACROSS, BESIDE)),
+    6: (1, (BESIDE, PARTNER)),
+    1: (1, (PARTNER,)),
+    3: (2, (ACROSS,)),
+    4: (2, (PARTNER,)),
+    7: (2, ()),
+    5: (3, ()),
+}
+CORNER = {
+    0: (0, (PARTNER, BESIDE)),
+    2: (1, (BESIDE,)),
+    1: (1, ()),
+    4: (2, (BESIDE,)),
+    3: (2, ()),
+    6: (3, (BESIDE,)),
+    5: (3, ()),
+    7: (4, ()),
+}
+SHIPPED = 0
+
+
+def grid_product(
+    rows, kernel_ref, slip_ref, total, held, slip_in, kernel_in, shipped, extra, returned,
+    links_send, links_recv, core_send, core_recv, back_send, back_recv, slip_sem, kernel_sem,
+):
+    members, columns = slip_ref.shape
+    width = columns // SLOTS
+    layers = rows // 4
+    me = lax.axis_index("row")
+    core = lax.rem(me, 2)
+    other = me + 1 - 2 * core
+    chip = me // 2
+    side = chip % 2
+    layer = chip // 2
+    flipped = layer + 1 - 2 * (layer % 2)
+    distance = (layer, flipped, (layer + layers // 2) % layers, layers - 1 - layer)
+    outer = layer * (layers - 1 - layer) == 0
+    inner = jnp.logical_not(outer)
+    away = jnp.where(outer, 1, 0)
+
+    def row_of(code):
+        beside = side + (1 - 2 * side) * (code % 2)
+        return (distance[code // 2] * 2 + beside) * 2 + core
+
+    def ships(parity):
+        return width // 8 * (1 + parity)
+
+    def keeps(parity):
+        return width - ships(parity)
+
+    pair_ships = ships(0) + ships(1)
+    pair_keeps = keeps(0) + keeps(1)
+
+    def block(ref, row, chunk, span):
+        return ref.at[
+            pl.ds(pl.multiple_of(row * members, members), members),
+            pl.ds(pl.multiple_of(chunk * width, width), span),
+        ]
+
+    def source(code, chunk, span):
+        if code == 0:
+            return slip_ref.at[:, pl.ds(pl.multiple_of(chunk * width, width), span)]
+        return block(held, row_of(code), chunk, span)
+
+    def sized(count, span):
+        return held.at[pl.ds(0, count), pl.ds(0, span)]
+
+    def send(code, link, chunk, span, lane):
+        pltpu.make_async_remote_copy(
+            src_ref=source(code, chunk, span),
+            dst_ref=block(held, row_of(code), chunk, span),
+            send_sem=links_send.at[lane],
+            recv_sem=links_recv.at[code ^ link, chunk],
+            device_id={"row": row_of(link)},
+            device_id_type=MESH,
+        ).start()
+
+    def arrive(code, chunk, span):
+        piece = block(held, row_of(code), chunk, span)
+        pltpu.make_async_copy(piece, piece, links_recv.at[code, chunk]).wait()
+
+    def pass_core(code, chunk, span):
+        pltpu.make_async_remote_copy(
+            src_ref=source(code, chunk, span),
+            dst_ref=block(held, row_of(code), chunk, span),
+            send_sem=core_send,
+            recv_sem=core_recv.at[chunk],
+            device_id={"row": other},
+            device_id_type=MESH,
+        ).start()
+
+    def ship_place(chunk, parity):
+        start = chunk // 2 * pair_ships + parity * ships(0)
+        return shipped.at[:, pl.ds(pl.multiple_of(start, LANES), ships(parity))]
+
+    def ship(chunk, parity):
+        start = chunk * width + keeps(parity)
+        return pltpu.make_async_remote_copy(
+            src_ref=kernel_ref.at[:, pl.ds(pl.multiple_of(start, LANES), ships(parity))],
+            dst_ref=ship_place(chunk, parity),
+            send_sem=links_send.at[4],
+            recv_sem=links_recv.at[SHIPPED, chunk],
+            device_id={"row": row_of(PARTNER)},
+            device_id_type=MESH,
+        )
+
+    def ship_arrive(chunk, parity):
+        piece = ship_place(chunk, parity)
+        pltpu.make_async_copy(piece, piece, links_recv.at[SHIPPED, chunk]).wait()
+
+    def move(table, chunk_at, parity, full):
+        for code, (hops, links) in table.items():
+            chunk = chunk_at - LAG * hops
+
+            @pl.when((chunk >= 0) & (chunk < SLOTS))
+            def _():
+                mine = width if full else keeps(parity)
+                if code:
+                    arrive(code, chunk, mine)
+                for link in links:
+                    if full and link == PARTNER:
+                        if code != 1:
+                            send(code, link, chunk, keeps(parity), 2)
+                        elif parity == 1:
+                            send(code, link, chunk, keeps(parity), 3)
+                    elif full:
+                        send(code, link, chunk, width, 0 if link == ACROSS else 1)
+                    elif link == PARTNER:
+                        send(code, link, chunk, width, 0)
+                    elif code != 2:
+                        send(code, link, chunk, keeps(parity), 2)
+                    elif parity == 0:
+                        send(code, link, chunk, keeps(parity), 3)
+                pass_core(code, chunk, mine)
+
+    def load_start(chunk, slot):
+        def place_in(row):
+            return slip_in.at[slot, pl.ds(pl.multiple_of(row * members, members), members)]
+
+        pltpu.make_async_copy(
+            source(0, chunk, width), place_in(me), slip_sem.at[slot]
+        ).start()
+
+        def one(at, carry):
+            row = (me + at) % rows
+            pltpu.make_async_copy(
+                block(held, row, chunk, width), place_in(row), slip_sem.at[slot]
+            ).start()
+            return carry
+
+        lax.fori_loop(1, rows, one, 0)
+
+    def slip_wait(slot):
+        pltpu.make_async_copy(
+            held.at[:, pl.ds(0, width)], slip_in.at[slot], slip_sem.at[slot]
+        ).wait()
+
+    def kernel_load(chunk, slot):
+        return pltpu.make_async_copy(
+            kernel_ref.at[:, pl.ds(pl.multiple_of(chunk * width, width), width)],
+            kernel_in.at[slot],
+            kernel_sem.at[slot],
+        )
+
+    def three(left, right):
+        l_high, l_low = left
+        r_high, r_low = right
+        return times(l_high, r_high) + (times(l_high, r_low) + times(l_low, r_high))
+
+    def product(chunk, slot, parity):
+        depth = ships(1)
+        whole = keeps(parity) // depth * depth
+
+        def one(at, carry):
+            span = pl.ds(pl.multiple_of(at * depth, depth), depth)
+            total[...] += three(split(kernel_in[slot, :, span]), split(slip_in[slot, :, span]))
+            return carry
+
+        lax.fori_loop(0, whole // depth, one, 0)
+        if keeps(parity) > whole:
+            span = pl.ds(whole, keeps(parity) - whole)
+            total[...] += three(split(kernel_in[slot, :, span]), split(slip_in[slot, :, span]))
+
+        @pl.when(inner)
+        def _():
+            ship_arrive(chunk, parity)
+            span = pl.ds(keeps(parity), ships(parity))
+            slips = split(slip_in[slot, :, span])
+            total[...] += three(split(kernel_in[slot, :, span]), slips)
+            start = chunk // 2 * pair_ships + parity * ships(0)
+            there = pl.ds(pl.multiple_of(start, LANES), ships(parity))
+            extra[...] += three(split(shipped[:, there]), slips)
+
+    total[...] = jnp.zeros_like(total)
+    extra[...] = jnp.zeros_like(extra)
+    last_hop = 3 + away
+
+    def step(at, parity):
+        @pl.when(inner)
+        def _():
+            move(MIDDLE, at, parity, True)
+
+        @pl.when(outer)
+        def _():
+            move(CORNER, at, parity, False)
+            ready = at - KERNEL_LAG
+
+            @pl.when((ready >= 0) & (ready < SLOTS))
+            def _():
+                ship(ready, parity).start()
+
+        done = at - LAG * last_hop
+        following = done - 1
+        current = done - 2
+
+        @pl.when((following >= 0) & (following < SLOTS))
+        def _():
+            slot = 1 - parity
+            kernel_load(following, slot).start()
+
+            @pl.when(inner)
+            def _():
+                piece = sized(members * rows // 2, width)
+                pltpu.make_async_copy(piece, piece, core_recv.at[following]).wait()
+
+            @pl.when(outer)
+            def _():
+                piece = sized(members * rows // 2, keeps(1 - parity))
+                pltpu.make_async_copy(piece, piece, core_recv.at[following]).wait()
+
+            load_start(following, slot)
+
+        @pl.when((current >= 0) & (current < SLOTS))
+        def _():
+            kernel_load(current, parity).wait()
+            slip_wait(parity)
+            product(current, parity, parity)
+
+    def travel(pair, carry):
+        for parity in range(2):
+            step(2 * pair + parity, parity)
+        return carry
+
+    lax.fori_loop(0, (SLOTS + 4 * LAG + 2) // 2, travel, 0)
+
+    def drained(piece, semaphore):
+        pltpu.make_async_copy(piece, piece, semaphore).wait()
+
+    back = pltpu.make_async_remote_copy(
+        src_ref=extra,
+        dst_ref=returned,
+        send_sem=back_send,
+        recv_sem=back_recv,
+        device_id={"row": row_of(PARTNER)},
+        device_id_type=MESH,
+    )
+    kept = SLOTS // 2 * pair_keeps
+
+    @pl.when(inner)
+    def _():
+        back.start()
+        drained(sized(3 * members, columns), links_send.at[0])
+        drained(sized(3 * members, columns), links_send.at[1])
+        drained(sized(3 * members, kept), links_send.at[2])
+        drained(sized(members, SLOTS // 2 * keeps(1)), links_send.at[3])
+        drained(sized(members * rows // 2, columns), core_send)
+        back.wait_send()
+
+    @pl.when(outer)
+    def _():
+        drained(sized(members, columns), links_send.at[0])
+        drained(sized(3 * members, kept), links_send.at[2])
+        drained(sized(members, SLOTS // 2 * keeps(0)), links_send.at[3])
+        drained(shipped, links_send.at[4])
+        drained(sized(members * rows // 2, kept), core_send)
+        back.wait_recv()
+        total[...] += returned[...]
+
+
+def grid_partial(rows, kernel, slip):
+    targets, columns = kernel.shape
+    members = slip.shape[0] * rows
+    width = columns // SLOTS
+    away = SLOTS // 2 * (width // 8 * 3)
+    dma = pltpu.SemaphoreType.DMA
+    return pl.pallas_call(
+        functools.partial(grid_product, rows),
+        out_shape=(
+            jax.ShapeDtypeStruct((targets, members), jnp.float32),
+            jax.ShapeDtypeStruct((members, columns), jnp.float32),
+        ),
+        in_specs=[pl.BlockSpec(memory_space=pl.ANY)] * 2,
+        out_specs=(pl.BlockSpec(memory_space=pltpu.VMEM), pl.BlockSpec(memory_space=pl.ANY)),
+        scratch_shapes=[
+            pltpu.VMEM((2, members, width), jnp.float32),
+            pltpu.VMEM((2, targets, width), jnp.float32),
+            pltpu.VMEM((targets, away), jnp.float32),
+            pltpu.VMEM((targets, members), jnp.float32),
+            pltpu.VMEM((targets, members), jnp.float32),
+            dma((5,)),
+            dma((8, SLOTS)),
+            dma,
+            dma((SLOTS,)),
+            dma,
+            dma,
+            dma((2,)),
+            dma((2,)),
+        ],
+        compiler_params=pltpu.CompilerParams(
+            has_side_effects=True, vmem_limit_bytes=48 * 1024 * 1024
+        ),
+        cost_estimate=pl.CostEstimate(
+            flops=6 * targets * members * columns,
+            bytes_accessed=4 * members * columns * 4,
+            transcendentals=0,
+        ),
+    )(kernel, slip)[0]
+
+
+def partial_sums(rows, kernel, slip):
+    if rows // 4 == 4 and kernel.shape[1] % (SLOTS * 8 * LANES) == 0:
+        return grid_partial(rows, kernel, slip)
+    return traction_partial(rows, kernel, slip)
+
+
 def add_over_columns(partial_value, columns):
     if columns != 2:
         return lax.psum_scatter(partial_value, "col", scatter_dimension=0, tiled=True)
@@ -270,7 +602,7 @@
 
 
 def per_device(rows, columns, kernel, slip, segment, prestress, state, normal_stress, a_table, b_table):
-    traction = add_over_columns(traction_partial(rows, kernel, slip), columns)
+    traction = add_over_columns(partial_sums(rows, kernel, slip), columns)
     return friction(traction, segment, prestress, state, normal_stress, a_table, b_table)
 
 

time: 350 us -> 324 us (0.926)
  Pallas kernels: 335 us -> 311 us
    pallas_call x1, Pallas kernels: 335 us -> 311 us  [grid_partial(): pl.pallas_call(functools.partial(grid_product, rows), out_shape=(jax.Shap...]
where the time goes in v1:
time: 324 us
  Pallas kernels  311 us (96%)
  waiting for transfers between devices  6.54 us (2%)
    pallas_call x1, Pallas kernels, grid_partial(): pl.pallas_call(functools.partial(grid_product, rows), out_shape=(jax.Shap...  311 us
    ppermute x1, waiting for transfers between devices, add_over_columns(): return mine + lax.ppermute(theirs, 'col', [(0, 1), (1, 0)])  6.54 us
  transfers between devices with their start and end apart: 1, of which 1 were waited for; matrix products, arithmetic and copies ran while one was open for 0% of the time, Pallas kernels for 0%

profile of v1, /device:TPU:0, one launch (start us, length us, event | category | flops | bytes accessed | tf_op | source)
XLA Modules:
  0.0 324.1 jit_solution(6910817124149875986)
XLA Ops:
  0.6 0.0 copy-start
  0.7 0.0 copy-start.1
  0.7 2.2 copy-done.1
  2.8 0.0 copy-start.5
  2.8 0.0 copy-start.6
  2.8 0.0 copy-start.4
  2.8 0.0 copy-start.2
  2.9 0.0 copy-start.3
  2.9 311.3 %shard_map.95 = (f32[320,512]{1,0:T(8,128)S(1)}, f32[512,32768]{1,0:T(8,128)}) custom-call(f32[320,32768]{1,0:T(8,128)} %kernel_ref.1, f32[32,32768]{1,0:T(8,128)S(1)} %copy-done.1), custom_call_target="tpu_custom_call" | custom-call | flops 32212254720 | bytes 268435456 | tf_op jit(solution)/shard_map/pallas_call | solution.py:540
  314.2 1.5 collective-permute-start
  315.7 0.0 copy-done
  315.7 0.0 copy-done.5
  315.7 0.2 fusion.4
  315.9 0.0 copy-done.6
  315.9 0.3 fusion.3
  316.2 0.0 copy-done.4
  316.2 0.1 divide_negate_fusion
  316.3 6.5 %collective-permute-done = f32[160,512]{1,0:T(8,128)S(1)} collective-permute-done((f32[160,512]{1,0:T(8,128)S(1)}, f32[160,512]{1,0:T(8,128)S(1)}, u32[]{:S(2)}, u32[]{:S(2)}) %collective-permute-start) | collective-permute-done | bytes 327712 | tf_op jit(solution)/shard_map/ppermute | solution.py:587
  322.8 0.0 copy-done.2
  322.8 0.0 copy-done.3
  322.8 1.3 multiply_add_fusion
  (1 shorter events, 0.0 us)
Async XLA Ops:
  0.6 315.1 %copy-start = (f32[16]{0:T(128)S(1)}, f32[16]{0:T(128)}, u32[]{:S(2)}) copy-start(f32[16]{0:T(128)} %param.15) | copy-start | bytes 196
  0.7 2.2 copy-start.1
  2.8 312.9 %copy-start.5 = (s32[160]{0:T(256)S(1)}, s32[160]{0:T(256)}, u32[]{:S(2)}) copy-start(s32[160]{0:T(256)} %param.10) | copy-start | bytes 1924
  2.8 313.1 %copy-start.6 = (f32[16]{0:T(128)S(1)}, f32[16]{0:T(128)}, u32[]{:S(2)}) copy-start(f32[16]{0:T(128)} %param.14) | copy-start | bytes 196
  2.8 313.4 %copy-start.4 = (f32[160]{0:T(256)S(1)}, f32[160]{0:T(256)}, u32[]{:S(2)}) copy-start(f32[160]{0:T(256)} %param.13) | copy-start | bytes 1924
  2.8 320.0 %copy-start.2 = (f32[160,512]{1,0:T(8,128)S(1)}, f32[160,512]{1,0:T(8,128)}, u32[]{:S(2)}) copy-start(f32[160,512]{1,0:T(8,128)} %param.12) | copy-start | bytes 983044
  2.9 320.0 %copy-start.3 = (f32[160,512]{1,0:T(8,128)S(1)}, f32[160,512]{1,0:T(8,128)}, u32[]{:S(2)}) copy-start(f32[160,512]{1,0:T(8,128)} %param.11) | copy-start | bytes 983044
  314.2 8.6 %collective-permute-start = (f32[160,512]{1,0:T(8,128)S(1)}, f32[160,512]{1,0:T(8,128)S(1)}, u32[]{:S(2)}, u32[]{:S(2)}) collective-permute-start(f32[160,512]{1,0:T(8,128)S(1)} %constant_dynamic-slice_fusion), channel_id=1, source_target_pairs={{0,1},{1,0},{2,3},{3,2},{4,5},{5,4},{6,7},{7,6},{8,9},{9,8},{10,11... | collective-permute-start | bytes 983048 | tf_op jit(solution)/shard_map/ppermute | solution.py:587

commit v2 on v1

--- a/solution.py
+++ b/solution.py
@@ -245,13 +245,23 @@
     )(kernel, slip)[0]
 
 
-BESIDE, PARTNER, ACROSS = 1, 2, 6
+def add_over_columns(partial_value, columns):
+    if columns != 2:
+        return lax.psum_scatter(partial_value, "col", scatter_dimension=0, tiled=True)
+    half = partial_value.shape[0] // 2
+    me = lax.axis_index("col")
+    mine = lax.dynamic_slice_in_dim(partial_value, me * half, half, 0)
+    theirs = lax.dynamic_slice_in_dim(partial_value, (1 - me) * half, half, 0)
+    return mine + lax.ppermute(theirs, "col", [(0, 1), (1, 0)])
+
+
+BESIDE, PARTNER, ACROSS, FAR = 1, 2, 6, 4
 SLOTS = 32
-LAG = 2
-KERNEL_LAG = 4
+LAG = 1
+AHEAD = 8
+KERNEL_LAG = 0
 LANES = 128
 MIDDLE = {
-    0: (0, (ACROSS, BESIDE, PARTNER)),
     2: (1, (ACROSS, BESIDE)),
     6: (1, (BESIDE, PARTNER)),
     1: (1, (PARTNER,)),
@@ -259,9 +269,9 @@
     4: (2, (PARTNER,)),
     7: (2, ()),
     5: (3, ()),
+    0: (0, (ACROSS, BESIDE, PARTNER)),
 }
 CORNER = {
-    0: (0, (PARTNER, BESIDE)),
     2: (1, (BESIDE,)),
     1: (1, ()),
     4: (2, (BESIDE,)),
@@ -269,28 +279,35 @@
     6: (3, (BESIDE,)),
     5: (3, ()),
     7: (4, ()),
+    0: (0, (PARTNER, BESIDE)),
 }
 SHIPPED = 0
 
 
 def grid_product(
-    rows, kernel_ref, slip_ref, total, held, slip_in, kernel_in, shipped, extra, returned,
-    links_send, links_recv, core_send, core_recv, back_send, back_recv, slip_sem, kernel_sem,
+    rows, kernel_ref, slip_ref, out, held, slip_in, kernel_in, shipped, total, extra, crossed,
+    returned, links_send, links_recv, core_send, core_recv, back_send, back_recv, pair_send,
+    pair_recv, slip_sem, kernel_sem,
 ):
     members, columns = slip_ref.shape
     width = columns // SLOTS
     layers = rows // 4
+    half = out.shape[0]
     me = lax.axis_index("row")
+    column = lax.axis_index("col")
     core = lax.rem(me, 2)
     other = me + 1 - 2 * core
     chip = me // 2
     side = chip % 2
     layer = chip // 2
+    end = layer // (layers // 2)
     flipped = layer + 1 - 2 * (layer % 2)
     distance = (layer, flipped, (layer + layers // 2) % layers, layers - 1 - layer)
     outer = layer * (layers - 1 - layer) == 0
     inner = jnp.logical_not(outer)
-    away = jnp.where(outer, 1, 0)
+    halves = (end, 1 - end)
+    far_lag = jnp.where(outer, 4 * LAG, 3 * LAG + 3 * LAG % 2)
+    lags = (2 * LAG, far_lag)
 
     def row_of(code):
         beside = side + (1 - 2 * side) * (code % 2)
@@ -318,6 +335,9 @@
 
     def sized(count, span):
         return held.at[pl.ds(0, count), pl.ds(0, span)]
+
+    def drained(piece, semaphore):
+        pltpu.make_async_copy(piece, piece, semaphore).wait()
 
     def send(code, link, chunk, span, lane):
         pltpu.make_async_remote_copy(
@@ -330,15 +350,14 @@
         ).start()
 
     def arrive(code, chunk, span):
-        piece = block(held, row_of(code), chunk, span)
-        pltpu.make_async_copy(piece, piece, links_recv.at[code, chunk]).wait()
+        drained(block(held, row_of(code), chunk, span), links_recv.at[code, chunk])
 
     def pass_core(code, chunk, span):
         pltpu.make_async_remote_copy(
             src_ref=source(code, chunk, span),
             dst_ref=block(held, row_of(code), chunk, span),
             send_sem=core_send,
-            recv_sem=core_recv.at[chunk],
+            recv_sem=core_recv.at[code // FAR, chunk],
             device_id={"row": other},
             device_id_type=MESH,
         ).start()
@@ -358,62 +377,75 @@
             device_id_type=MESH,
         )
 
-    def ship_arrive(chunk, parity):
-        piece = ship_place(chunk, parity)
-        pltpu.make_async_copy(piece, piece, links_recv.at[SHIPPED, chunk]).wait()
-
-    def move(table, chunk_at, parity, full):
+    def pass_on(code, links, chunk, parity, full):
+        if code:
+            arrive(code, chunk, width if full else keeps(parity))
+        for link in links:
+            if full and link == PARTNER:
+                if code != 1:
+                    send(code, link, chunk, keeps(parity), 2)
+                elif parity == 1:
+                    send(code, link, chunk, keeps(parity), 3)
+            elif full:
+                send(code, link, chunk, width, 0 if link == ACROSS else 1)
+            elif link == PARTNER:
+                send(code, link, chunk, width, 0)
+            elif code != 2:
+                send(code, link, chunk, keeps(parity), 2)
+            elif parity == 0:
+                send(code, link, chunk, keeps(parity), 3)
+        pass_core(code, chunk, width if full else keeps(parity))
+
+    def move(table, at, parity, full):
         for code, (hops, links) in table.items():
-            chunk = chunk_at - LAG * hops
+            late = LAG * hops if code else -AHEAD
+            chunk = at - late
 
             @pl.when((chunk >= 0) & (chunk < SLOTS))
             def _():
-                mine = width if full else keeps(parity)
-                if code:
-                    arrive(code, chunk, mine)
-                for link in links:
-                    if full and link == PARTNER:
-                        if code != 1:
-                            send(code, link, chunk, keeps(parity), 2)
-                        elif parity == 1:
-                            send(code, link, chunk, keeps(parity), 3)
-                    elif full:
-                        send(code, link, chunk, width, 0 if link == ACROSS else 1)
-                    elif link == PARTNER:
-                        send(code, link, chunk, width, 0)
-                    elif code != 2:
-                        send(code, link, chunk, keeps(parity), 2)
-                    elif parity == 0:
-                        send(code, link, chunk, keeps(parity), 3)
-                pass_core(code, chunk, mine)
-
-    def load_start(chunk, slot):
-        def place_in(row):
-            return slip_in.at[slot, pl.ds(pl.multiple_of(row * members, members), members)]
+                pass_on(code, links, chunk, (parity + late) % 2, full)
+
+    def load_start(part, chunk, slot):
+        into = slip_in.at[part, slot]
+        if part:
+            pltpu.make_async_copy(
+                held.at[
+                    pl.ds(pl.multiple_of(halves[1] * (rows // 2 * members), members), rows // 2 * members),
+                    pl.ds(pl.multiple_of(chunk * width, width), width),
+                ],
+                into,
+                slip_sem.at[part, slot],
+            ).start()
+            return
+        first = end * (rows // 2)
+        mine = me - first
+
+        def place_in(spot):
+            return into.at[pl.ds(pl.multiple_of(spot * members, members), members)]
 
         pltpu.make_async_copy(
-            source(0, chunk, width), place_in(me), slip_sem.at[slot]
+            source(0, chunk, width), place_in(mine), slip_sem.at[part, slot]
         ).start()
 
         def one(at, carry):
-            row = (me + at) % rows
+            spot = (mine + at) % (rows // 2)
             pltpu.make_async_copy(
-                block(held, row, chunk, width), place_in(row), slip_sem.at[slot]
+                block(held, first + spot, chunk, width), place_in(spot), slip_sem.at[part, slot]
             ).start()
             return carry
 
-        lax.fori_loop(1, rows, one, 0)
-
-    def slip_wait(slot):
+        lax.fori_loop(1, rows // 2, one, 0)
+
+    def slip_wait(part, slot):
         pltpu.make_async_copy(
-            held.at[:, pl.ds(0, width)], slip_in.at[slot], slip_sem.at[slot]
+            sized(rows // 2 * members, width), slip_in.at[part, slot], slip_sem.at[part, slot]
         ).wait()
 
-    def kernel_load(chunk, slot):
+    def kernel_load(part, chunk, slot):
         return pltpu.make_async_copy(
             kernel_ref.at[:, pl.ds(pl.multiple_of(chunk * width, width), width)],
-            kernel_in.at[slot],
-            kernel_sem.at[slot],
+            kernel_in.at[part, slot],
+            kernel_sem.at[part, slot],
         )
 
     def three(left, right):
@@ -421,33 +453,71 @@
         r_high, r_low = right
         return times(l_high, r_high) + (times(l_high, r_low) + times(l_low, r_high))
 
-    def product(chunk, slot, parity):
+    def product(part, chunk, slot, parity):
         depth = ships(1)
         whole = keeps(parity) // depth * depth
+        where = halves[part]
+
+        def add(span):
+            total[where] += three(
+                split(kernel_in[part, slot, :, span]), split(slip_in[part, slot, :, span])
+            )
 
         def one(at, carry):
-            span = pl.ds(pl.multiple_of(at * depth, depth), depth)
-            total[...] += three(split(kernel_in[slot, :, span]), split(slip_in[slot, :, span]))
+            add(pl.ds(pl.multiple_of(at * depth, depth), depth))
             return carry
 
         lax.fori_loop(0, whole // depth, one, 0)
         if keeps(parity) > whole:
-            span = pl.ds(whole, keeps(parity) - whole)
-            total[...] += three(split(kernel_in[slot, :, span]), split(slip_in[slot, :, span]))
+            add(pl.ds(whole, keeps(parity) - whole))
 
         @pl.when(inner)
         def _():
-            ship_arrive(chunk, parity)
+            if part == 0:
+                drained(ship_place(chunk, parity), links_recv.at[SHIPPED, chunk])
             span = pl.ds(keeps(parity), ships(parity))
-            slips = split(slip_in[slot, :, span])
-            total[...] += three(split(kernel_in[slot, :, span]), slips)
+            slips = split(slip_in[part, slot, :, span])
+            total[where] += three(split(kernel_in[part, slot, :, span]), slips)
             start = chunk // 2 * pair_ships + parity * ships(0)
             there = pl.ds(pl.multiple_of(start, LANES), ships(parity))
-            extra[...] += three(split(shipped[:, there]), slips)
+            extra[where] += three(split(shipped[:, there]), slips)
+
+    def rows_for(which):
+        return pl.ds(pl.multiple_of(which * half, half), half)
+
+    def exchange(part):
+        where = halves[part]
+        return pltpu.make_async_remote_copy(
+            src_ref=total.at[where, rows_for(1 - column)],
+            dst_ref=crossed.at[where],
+            send_sem=pair_send.at[part],
+            recv_sem=pair_recv.at[part],
+            device_id={"col": 1 - column},
+            device_id_type=MESH,
+        )
+
+    def give_back(part, turned):
+        where = halves[part]
+        target = 1 - column if turned else column
+        return pltpu.make_async_remote_copy(
+            src_ref=extra.at[where, rows_for(target)],
+            dst_ref=returned.at[turned, where],
+            send_sem=back_send.at[turned, part],
+            recv_sem=back_recv.at[turned, part],
+            device_id={"row": row_of(PARTNER), "col": target},
+            device_id_type=MESH,
+        )
+
+    def reduce_start(part):
+        @pl.when(inner)
+        def _():
+            for turned in range(2):
+                give_back(part, turned).start()
+
+        exchange(part).start()
 
     total[...] = jnp.zeros_like(total)
     extra[...] = jnp.zeros_like(extra)
-    last_hop = 3 + away
 
     def step(at, parity):
         @pl.when(inner)
@@ -463,62 +533,70 @@
             def _():
                 ship(ready, parity).start()
 
-        done = at - LAG * last_hop
-        following = done - 1
-        current = done - 2
-
-        @pl.when((following >= 0) & (following < SLOTS))
-        def _():
-            slot = 1 - parity
-            kernel_load(following, slot).start()
+        for part in range(2):
+            done = at - lags[part]
+            following = done - 1
+            current = done - 2
+
+            @pl.when((following >= 0) & (following < SLOTS))
+            def _():
+                slot = 1 - parity
+
+                @pl.when(inner)
+                def _():
+                    drained(sized(rows // 4 * members, width), core_recv.at[part, following])
+
+                @pl.when(outer)
+                def _():
+                    drained(sized(rows // 4 * members, keeps(slot)), core_recv.at[part, following])
+
+                load_start(part, following, slot)
+
+            @pl.when((current >= 0) & (current < SLOTS))
+            def _():
+                kernel_load(part, current, parity).wait()
+                slip_wait(part, parity)
+                product(part, current, parity, parity)
+
+            @pl.when((done >= 0) & (done < SLOTS))
+            def _():
+                kernel_load(part, done, parity).start()
+
+            @pl.when(current == SLOTS)
+            def _():
+                reduce_start(part)
+
+    def begin(pair, carry):
+        for parity in range(2):
+            chunk = 2 * pair + parity
 
             @pl.when(inner)
             def _():
-                piece = sized(members * rows // 2, width)
-                pltpu.make_async_copy(piece, piece, core_recv.at[following]).wait()
+                pass_on(0, MIDDLE[0][1], chunk, parity, True)
 
             @pl.when(outer)
             def _():
-                piece = sized(members * rows // 2, keeps(1 - parity))
-                pltpu.make_async_copy(piece, piece, core_recv.at[following]).wait()
-
-            load_start(following, slot)
-
-        @pl.when((current >= 0) & (current < SLOTS))
-        def _():
-            kernel_load(current, parity).wait()
-            slip_wait(parity)
-            product(current, parity, parity)
+                pass_on(0, CORNER[0][1], chunk, parity, False)
+
+        return carry
 
     def travel(pair, carry):
         for parity in range(2):
             step(2 * pair + parity, parity)
         return carry
 
-    lax.fori_loop(0, (SLOTS + 4 * LAG + 2) // 2, travel, 0)
-
-    def drained(piece, semaphore):
-        pltpu.make_async_copy(piece, piece, semaphore).wait()
-
-    back = pltpu.make_async_remote_copy(
-        src_ref=extra,
-        dst_ref=returned,
-        send_sem=back_send,
-        recv_sem=back_recv,
-        device_id={"row": row_of(PARTNER)},
-        device_id_type=MESH,
-    )
+    lax.fori_loop(0, AHEAD // 2, begin, 0)
+    lax.fori_loop(0, (SLOTS + 4 * LAG + 4) // 2, travel, 0)
+
     kept = SLOTS // 2 * pair_keeps
 
     @pl.when(inner)
     def _():
-        back.start()
         drained(sized(3 * members, columns), links_send.at[0])
         drained(sized(3 * members, columns), links_send.at[1])
         drained(sized(3 * members, kept), links_send.at[2])
         drained(sized(members, SLOTS // 2 * keeps(1)), links_send.at[3])
         drained(sized(members * rows // 2, columns), core_send)
-        back.wait_send()
 
     @pl.when(outer)
     def _():
@@ -527,11 +605,32 @@
         drained(sized(members, SLOTS // 2 * keeps(0)), links_send.at[3])
         drained(shipped, links_send.at[4])
         drained(sized(members * rows // 2, kept), core_send)
-        back.wait_recv()
-        total[...] += returned[...]
-
-
-def grid_partial(rows, kernel, slip):
+
+    span = out.shape[1] // 2
+    for part in range(2):
+        exchange(part).wait_recv()
+    for where in range(2):
+        out[:, pl.ds(where * span, span)] = total[where, rows_for(column)] + crossed[where]
+
+    @pl.when(outer)
+    def _():
+        for part in range(2):
+            for turned in range(2):
+                give_back(part, turned).wait_recv()
+        for where in range(2):
+            out[:, pl.ds(where * span, span)] += returned[0, where] + returned[1, where]
+
+    for part in range(2):
+        exchange(part).wait_send()
+
+    @pl.when(inner)
+    def _():
+        for part in range(2):
+            for turned in range(2):
+                give_back(part, turned).wait_send()
+
+
+def grid_traction(rows, kernel, slip):
     targets, columns = kernel.shape
     members = slip.shape[0] * rows
     width = columns // SLOTS
@@ -540,25 +639,29 @@
     return pl.pallas_call(
         functools.partial(grid_product, rows),
         out_shape=(
-            jax.ShapeDtypeStruct((targets, members), jnp.float32),
+            jax.ShapeDtypeStruct((targets // 2, members), jnp.float32),
             jax.ShapeDtypeStruct((members, columns), jnp.float32),
         ),
         in_specs=[pl.BlockSpec(memory_space=pl.ANY)] * 2,
         out_specs=(pl.BlockSpec(memory_space=pltpu.VMEM), pl.BlockSpec(memory_space=pl.ANY)),
         scratch_shapes=[
-            pltpu.VMEM((2, members, width), jnp.float32),
-            pltpu.VMEM((2, targets, width), jnp.float32),
+            pltpu.VMEM((2, 2, members // 2, width), jnp.float32),
+            pltpu.VMEM((2, 2, targets, width), jnp.float32),
             pltpu.VMEM((targets, away), jnp.float32),
-            pltpu.VMEM((targets, members), jnp.float32),
-            pltpu.VMEM((targets, members), jnp.float32),
+            pltpu.VMEM((2, targets, members // 2), jnp.float32),
+            pltpu.VMEM((2, targets, members // 2), jnp.float32),
+            pltpu.VMEM((2, targets // 2, members // 2), jnp.float32),
+            pltpu.VMEM((2, 2, targets // 2, members // 2), jnp.float32),
             dma((5,)),
             dma((8, SLOTS)),
             dma,
-            dma((SLOTS,)),
-            dma,
-            dma,
+            dma((2, SLOTS)),
+            dma((2, 2)),
+            dma((2, 2)),
             dma((2,)),
             dma((2,)),
+            dma((2, 2)),
+            dma((2, 2)),
         ],
         compiler_params=pltpu.CompilerParams(
             has_side_effects=True, vmem_limit_bytes=48 * 1024 * 1024
@@ -571,20 +674,10 @@
     )(kernel, slip)[0]
 
 
-def partial_sums(rows, kernel, slip):
-    if rows // 4 == 4 and kernel.shape[1] % (SLOTS * 8 * LANES) == 0:
-        return grid_partial(rows, kernel, slip)
-    return traction_partial(rows, kernel, slip)
-
-
-def add_over_columns(partial_value, columns):
-    if columns != 2:
-        return lax.psum_scatter(partial_value, "col", scatter_dimension=0, tiled=True)
-    half = partial_value.shape[0] // 2
-    me = lax.axis_index("col")
-    mine = lax.dynamic_slice_in_dim(partial_value, me * half, half, 0)
-    theirs = lax.dynamic_slice_in_dim(partial_value, (1 - me) * half, half, 0)
-    return mine + lax.ppermute(theirs, "col", [(0, 1), (1, 0)])
+def traction_rows(rows, columns, kernel, slip):
+    if rows // 4 == 4 and columns == 2 and kernel.shape[1] % (SLOTS * 8 * LANES) == 0:
+        return grid_traction(rows, kernel, slip)
+    return add_over_columns(traction_partial(rows, kernel, slip), columns)
 
 
 def friction(traction, segment, prestress, state, normal_stress, a_table, b_table):
@@ -602,7 +695,7 @@
 
 
 def per_device(rows, columns, kernel, slip, segment, prestress, state, normal_stress, a_table, b_table):
-    traction = add_over_columns(partial_sums(rows, kernel, slip), columns)
+    traction = traction_rows(rows, columns, kernel, slip)
     return friction(traction, segment, prestress, state, normal_stress, a_table, b_table)
 
 

time: 324 us -> 317 us (0.978)
  waiting for transfers between devices: 6.54 us -> 0 us
    ppermute x1 -> x0, waiting for transfers between devices: 6.54 us -> none  [add_over_columns(): return mine + lax.ppermute(theirs, 'col', [(0, 1), (1, 0)])]
  transfers between devices with their start and end apart: 1 -> 0, of which waited for: 1 -> 0; matrix products, arithmetic and copies ran while one was open for 0% -> 0% of each run, Pallas kernels for 0% -> 0%
where the time goes in v2:
time: 317 us; the launch traced here: 316 us
  Pallas kernels  309 us (97%)
    pallas_call x1, Pallas kernels, grid_traction(): pl.pallas_call(functools.partial(grid_product, rows), out_shape=(jax.Shap...  309 us

profile of v2, /device:TPU:0, one launch (start us, length us, event | category | flops | bytes accessed | tf_op | source)
XLA Modules:
  0.0 316.4 jit_solution(1763751853331669452)
XLA Ops:
  0.6 0.0 copy-start
  0.6 0.6 copy-done
  1.3 0.9 fusion.3
  2.2 1.0 fusion.4
  3.1 0.8 divide_negate_fusion
  3.9 0.0 copy-start.1
  3.9 2.2 copy-done.1
  6.1 0.0 copy-start.2
  6.1 0.0 copy-start.3
  6.1 309.0 %shard_map.95 = (f32[160,512]{1,0:T(8,128)S(1)}, f32[512,32768]{1,0:T(8,128)}) custom-call(f32[320,32768]{1,0:T(8,128)} %kernel_ref.1, f32[32,32768]{1,0:T(8,128)S(1)} %copy-done.1), custom_call_target="tpu_custom_call" | custom-call | flops 32212254720 | bytes 268435456 | tf_op jit(solution)/shard_map/pallas_call | solution.py:639
  315.1 0.0 copy-done.2
  315.1 0.0 copy-done.3
  315.1 1.3 multiply_add_fusion
Async XLA Ops:
  0.6 0.7 copy-start
  3.9 2.2 copy-start.1
  6.1 309.0 %copy-start.2 = (f32[160,512]{1,0:T(8,128)S(1)}, f32[160,512]{1,0:T(8,128)}, u32[]{:S(2)}) copy-start(f32[160,512]{1,0:T(8,128)} %param.12) | copy-start | bytes 983044
  6.1 309.1 %copy-start.3 = (f32[160,512]{1,0:T(8,128)S(1)}, f32[160,512]{1,0:T(8,128)}, u32[]{:S(2)}) copy-start(f32[160,512]{1,0:T(8,128)} %param.11) | copy-start | bytes 983044

commit v3 on v2

--- a/solution.py
+++ b/solution.py
@@ -255,32 +255,46 @@
     return mine + lax.ppermute(theirs, "col", [(0, 1), (1, 0)])
 
 
-BESIDE, PARTNER, ACROSS, FAR = 1, 2, 6, 4
+BESIDE, PARTNER, ACROSS = 1, 2, 6
 SLOTS = 32
-LAG = 1
+LAG = 2
+EXTRA = 2
 AHEAD = 8
+OWN_LAG = -AHEAD
 KERNEL_LAG = 0
 LANES = 128
-MIDDLE = {
-    2: (1, (ACROSS, BESIDE)),
-    6: (1, (BESIDE, PARTNER)),
-    1: (1, (PARTNER,)),
-    3: (2, (ACROSS,)),
-    4: (2, (PARTNER,)),
-    7: (2, ()),
-    5: (3, ()),
-    0: (0, (ACROSS, BESIDE, PARTNER)),
-}
-CORNER = {
-    2: (1, (BESIDE,)),
-    1: (1, ()),
-    4: (2, (BESIDE,)),
-    3: (2, ()),
-    6: (3, (BESIDE,)),
-    5: (3, ()),
-    7: (4, ()),
-    0: (0, (PARTNER, BESIDE)),
-}
+SHIPS = (1, 2)
+DIRECT = (False, True)
+PHASES = len(SHIPS)
+MIDDLE = {2: LAG, 6: LAG, 1: LAG, 3: 2 * LAG, 4: 2 * LAG, 7: 2 * LAG + EXTRA, 5: 3 * LAG + EXTRA}
+CORNER = {2: LAG, 1: LAG, 4: 2 * LAG, 3: 2 * LAG, 6: 3 * LAG, 5: 3 * LAG, 7: 4 * LAG}
+MIDDLE_SENDS = (
+    (2, ACROSS, LAG),
+    (2, BESIDE, LAG),
+    (6, PARTNER, LAG),
+    (4, PARTNER, 2 * LAG),
+    (6, BESIDE, LAG + EXTRA),
+    (3, ACROSS, 2 * LAG + EXTRA),
+    (1, PARTNER, LAG),
+    (0, ACROSS, -AHEAD),
+    (0, BESIDE, -AHEAD),
+    (0, PARTNER, -AHEAD),
+)
+CORNER_SENDS = (
+    (6, BESIDE, 3 * LAG),
+    (4, BESIDE, 2 * LAG),
+    (2, BESIDE, LAG),
+    (0, PARTNER, -AHEAD),
+    (0, BESIDE, OWN_LAG),
+)
+MIDDLE_FAR, CORNER_FAR = (4, 5, 6, 7), (4, 5, 6, 7)
+MIDDLE_LAGS = tuple(
+    max(late for code, late in MIDDLE.items() if (code in MIDDLE_FAR) == far) for far in (False, True)
+)
+CORNER_LAGS = tuple(
+    max(late for code, late in CORNER.items() if (code in CORNER_FAR) == far) for far in (False, True)
+)
+LAGS = tuple(max(pair) for pair in zip(MIDDLE_LAGS, CORNER_LAGS))
 SHIPPED = 0
 
 
@@ -305,22 +319,24 @@
     distance = (layer, flipped, (layer + layers // 2) % layers, layers - 1 - layer)
     outer = layer * (layers - 1 - layer) == 0
     inner = jnp.logical_not(outer)
-    halves = (end, 1 - end)
-    far_lag = jnp.where(outer, 4 * LAG, 3 * LAG + 3 * LAG % 2)
-    lags = (2 * LAG, far_lag)
+    firsts = (end * (rows // 2), (1 - end) * (rows // 2))
+    counts = (rows // 2, rows // 2)
 
     def row_of(code):
         beside = side + (1 - 2 * side) * (code % 2)
         return (distance[code // 2] * 2 + beside) * 2 + core
 
-    def ships(parity):
-        return width // 8 * (1 + parity)
-
-    def keeps(parity):
-        return width - ships(parity)
-
-    pair_ships = ships(0) + ships(1)
-    pair_keeps = keeps(0) + keeps(1)
+    def ships(phase):
+        return width // 8 * SHIPS[phase]
+
+    def keeps(phase):
+        return width - ships(phase)
+
+    group_ships = sum(map(ships, range(PHASES)))
+    group_keeps = sum(map(keeps, range(PHASES)))
+    groups = SLOTS // PHASES
+    direct = groups * sum(keeps(phase) for phase in range(PHASES) if DIRECT[phase])
+    kept = groups * group_keeps
 
     def block(ref, row, chunk, span):
         return ref.at[
@@ -339,7 +355,20 @@
     def drained(piece, semaphore):
         pltpu.make_async_copy(piece, piece, semaphore).wait()
 
-    def send(code, link, chunk, span, lane):
+    def send(code, link, chunk, phase, full):
+        span, lane = keeps(phase), 2
+        if full and link != PARTNER:
+            span, lane = width, 0 if link == ACROSS else 1
+        elif full and code == 1:
+            if not DIRECT[phase]:
+                return
+            lane = 3
+        elif not full and link == PARTNER:
+            span, lane = width, 0
+        elif not full and code == 2:
+            if DIRECT[phase]:
+                return
+            lane = 3
         pltpu.make_async_remote_copy(
             src_ref=source(code, chunk, span),
             dst_ref=block(held, row_of(code), chunk, span),
@@ -349,76 +378,86 @@
             device_id_type=MESH,
         ).start()
 
-    def arrive(code, chunk, span):
-        drained(block(held, row_of(code), chunk, span), links_recv.at[code, chunk])
-
-    def pass_core(code, chunk, span):
+    def pass_core(code, chunk, span, part):
         pltpu.make_async_remote_copy(
             src_ref=source(code, chunk, span),
             dst_ref=block(held, row_of(code), chunk, span),
             send_sem=core_send,
-            recv_sem=core_recv.at[code // FAR, chunk],
+            recv_sem=core_recv.at[part, chunk],
             device_id={"row": other},
             device_id_type=MESH,
         ).start()
 
-    def ship_place(chunk, parity):
-        start = chunk // 2 * pair_ships + parity * ships(0)
-        return shipped.at[:, pl.ds(pl.multiple_of(start, LANES), ships(parity))]
-
-    def ship(chunk, parity):
-        start = chunk * width + keeps(parity)
-        return pltpu.make_async_remote_copy(
-            src_ref=kernel_ref.at[:, pl.ds(pl.multiple_of(start, LANES), ships(parity))],
-            dst_ref=ship_place(chunk, parity),
+    def ship_place(chunk, phase):
+        start = chunk // PHASES * group_ships + sum(map(ships, range(phase)))
+        return pl.ds(pl.multiple_of(start, LANES), ships(phase))
+
+    def ship(chunk, phase):
+        start = chunk * width + keeps(phase)
+        pltpu.make_async_remote_copy(
+            src_ref=kernel_ref.at[:, pl.ds(pl.multiple_of(start, LANES), ships(phase))],
+            dst_ref=shipped.at[:, ship_place(chunk, phase)],
             send_sem=links_send.at[4],
             recv_sem=links_recv.at[SHIPPED, chunk],
             device_id={"row": row_of(PARTNER)},
             device_id_type=MESH,
-        )
-
-    def pass_on(code, links, chunk, parity, full):
-        if code:
-            arrive(code, chunk, width if full else keeps(parity))
-        for link in links:
-            if full and link == PARTNER:
-                if code != 1:
-                    send(code, link, chunk, keeps(parity), 2)
-                elif parity == 1:
-                    send(code, link, chunk, keeps(parity), 3)
-            elif full:
-                send(code, link, chunk, width, 0 if link == ACROSS else 1)
-            elif link == PARTNER:
-                send(code, link, chunk, width, 0)
-            elif code != 2:
-                send(code, link, chunk, keeps(parity), 2)
-            elif parity == 0:
-                send(code, link, chunk, keeps(parity), 3)
-        pass_core(code, chunk, width if full else keeps(parity))
-
-    def move(table, at, parity, full):
-        for code, (hops, links) in table.items():
-            late = LAG * hops if code else -AHEAD
-            chunk = at - late
-
-            @pl.when((chunk >= 0) & (chunk < SLOTS))
-            def _():
-                pass_on(code, links, chunk, (parity + late) % 2, full)
+        ).start()
+
+    def at_chunk(at, phase, late, act):
+        chunk = at - late
+
+        @pl.when((chunk >= 0) & (chunk < SLOTS))
+        def _():
+            act(chunk, (phase - late) % PHASES)
+
+    def move(arrivals, sends, far, at, phase, full):
+        def span(phase):
+            return width if full else keeps(phase)
+
+        def sending(late, code=None):
+            chosen = [s for s in sends if s[2] == late and (code is None or s[0] == code)]
+
+            def act(chunk, phase):
+                for code, link, _ in chosen:
+                    send(code, link, chunk, phase, full)
+
+            if chosen:
+                at_chunk(at, phase, late, act)
+
+        for code, late in arrivals.items():
+
+            def act(chunk, phase):
+                piece = block(held, row_of(code), chunk, span(phase))
+                drained(piece, links_recv.at[code, chunk])
+                for forwarded, link, when in sends:
+                    if forwarded == code and when == late:
+                        send(code, link, chunk, phase, full)
+                pass_core(code, chunk, span(phase), int(code in far))
+
+            at_chunk(at, phase, late, act)
+        for code, link, when in sends:
+            if code and when != arrivals[code]:
+                at_chunk(
+                    at, phase, when, lambda chunk, phase: send(code, link, chunk, phase, full)
+                )
+        for code, link, when in sends:
+            if code == 0:
+                at_chunk(at, phase, when, lambda chunk, phase: send(0, link, chunk, phase, full))
+        at_chunk(at, phase, 0, lambda chunk, phase: pass_core(0, chunk, span(phase), 0))
 
     def load_start(part, chunk, slot):
-        into = slip_in.at[part, slot]
+        into = slip_in[part].at[slot]
         if part:
             pltpu.make_async_copy(
                 held.at[
-                    pl.ds(pl.multiple_of(halves[1] * (rows // 2 * members), members), rows // 2 * members),
+                    pl.ds(pl.multiple_of(firsts[1] * members, members), counts[1] * members),
                     pl.ds(pl.multiple_of(chunk * width, width), width),
                 ],
                 into,
                 slip_sem.at[part, slot],
             ).start()
             return
-        first = end * (rows // 2)
-        mine = me - first
+        mine = me - firsts[0]
 
         def place_in(spot):
             return into.at[pl.ds(pl.multiple_of(spot * members, members), members)]
@@ -428,17 +467,17 @@
         ).start()
 
         def one(at, carry):
-            spot = (mine + at) % (rows // 2)
+            spot = (mine + at) % counts[0]
             pltpu.make_async_copy(
-                block(held, first + spot, chunk, width), place_in(spot), slip_sem.at[part, slot]
+                block(held, firsts[0] + spot, chunk, width), place_in(spot), slip_sem.at[part, slot]
             ).start()
             return carry
 
-        lax.fori_loop(1, rows // 2, one, 0)
+        lax.fori_loop(1, counts[0], one, 0)
 
     def slip_wait(part, slot):
         pltpu.make_async_copy(
-            sized(rows // 2 * members, width), slip_in.at[part, slot], slip_sem.at[part, slot]
+            sized(counts[part] * members, width), slip_in[part].at[slot], slip_sem.at[part, slot]
         ).wait()
 
     def kernel_load(part, chunk, slot):
@@ -453,43 +492,35 @@
         r_high, r_low = right
         return times(l_high, r_high) + (times(l_high, r_low) + times(l_low, r_high))
 
-    def product(part, chunk, slot, parity):
-        depth = ships(1)
-        whole = keeps(parity) // depth * depth
-        where = halves[part]
-
-        def add(span):
-            total[where] += three(
-                split(kernel_in[part, slot, :, span]), split(slip_in[part, slot, :, span])
-            )
-
-        def one(at, carry):
-            add(pl.ds(pl.multiple_of(at * depth, depth), depth))
-            return carry
-
-        lax.fori_loop(0, whole // depth, one, 0)
-        if keeps(parity) > whole:
-            add(pl.ds(whole, keeps(parity) - whole))
+    def product(part, chunk, slot, phase):
+        def both(span):
+            return split(kernel_in[part, slot, :, span]), split(slip_in[part][slot, :, span])
+
+        depth = 2 * LANES
+        spans = [
+            pl.ds(start, min(depth, keeps(phase) - start)) for start in range(0, keeps(phase), depth)
+        ]
+        for span in spans:
+            total[part][...] += three(*both(span))
+        if not ships(phase):
+            return
 
         @pl.when(inner)
         def _():
+            there = ship_place(chunk, phase)
             if part == 0:
-                drained(ship_place(chunk, parity), links_recv.at[SHIPPED, chunk])
-            span = pl.ds(keeps(parity), ships(parity))
-            slips = split(slip_in[part, slot, :, span])
-            total[where] += three(split(kernel_in[part, slot, :, span]), slips)
-            start = chunk // 2 * pair_ships + parity * ships(0)
-            there = pl.ds(pl.multiple_of(start, LANES), ships(parity))
-            extra[where] += three(split(shipped[:, there]), slips)
+                drained(shipped.at[:, there], links_recv.at[SHIPPED, chunk])
+            kernels, slips = both(pl.ds(keeps(phase), ships(phase)))
+            total[part][...] += three(kernels, slips)
+            extra[part][...] += three(split(shipped[:, there]), slips)
 
     def rows_for(which):
         return pl.ds(pl.multiple_of(which * half, half), half)
 
     def exchange(part):
-        where = halves[part]
         return pltpu.make_async_remote_copy(
-            src_ref=total.at[where, rows_for(1 - column)],
-            dst_ref=crossed.at[where],
+            src_ref=total[part].at[rows_for(1 - column)],
+            dst_ref=crossed[part],
             send_sem=pair_send.at[part],
             recv_sem=pair_recv.at[part],
             device_id={"col": 1 - column},
@@ -497,11 +528,10 @@
         )
 
     def give_back(part, turned):
-        where = halves[part]
         target = 1 - column if turned else column
         return pltpu.make_async_remote_copy(
-            src_ref=extra.at[where, rows_for(target)],
-            dst_ref=returned.at[turned, where],
+            src_ref=extra[part].at[rows_for(target)],
+            dst_ref=returned[part].at[turned],
             send_sem=back_send.at[turned, part],
             recv_sem=back_recv.at[turned, part],
             device_id={"row": row_of(PARTNER), "col": target},
@@ -516,109 +546,122 @@
 
         exchange(part).start()
 
-    total[...] = jnp.zeros_like(total)
-    extra[...] = jnp.zeros_like(extra)
-
-    def step(at, parity):
+    for part in range(2):
+        total[part][...] = jnp.zeros_like(total[part])
+        extra[part][...] = jnp.zeros_like(extra[part])
+
+    def step(at, phase):
         @pl.when(inner)
         def _():
-            move(MIDDLE, at, parity, True)
+            move(MIDDLE, MIDDLE_SENDS, MIDDLE_FAR, at, phase, True)
 
         @pl.when(outer)
         def _():
-            move(CORNER, at, parity, False)
-            ready = at - KERNEL_LAG
-
-            @pl.when((ready >= 0) & (ready < SLOTS))
-            def _():
-                ship(ready, parity).start()
+            move(CORNER, CORNER_SENDS, CORNER_FAR, at, phase, False)
+
+            def act(chunk, phase):
+                if ships(phase):
+                    ship(chunk, phase)
+
+            at_chunk(at, phase, KERNEL_LAG, act)
 
         for part in range(2):
-            done = at - lags[part]
-            following = done - 1
-            current = done - 2
-
-            @pl.when((following >= 0) & (following < SLOTS))
-            def _():
-                slot = 1 - parity
+
+            def load(chunk, phase):
+                slot = phase % 2
 
                 @pl.when(inner)
                 def _():
-                    drained(sized(rows // 4 * members, width), core_recv.at[part, following])
+                    drained(sized(counts[part] // 2 * members, width), core_recv.at[part, chunk])
 
                 @pl.when(outer)
                 def _():
-                    drained(sized(rows // 4 * members, keeps(slot)), core_recv.at[part, following])
-
-                load_start(part, following, slot)
-
-            @pl.when((current >= 0) & (current < SLOTS))
-            def _():
-                kernel_load(part, current, parity).wait()
-                slip_wait(part, parity)
-                product(part, current, parity, parity)
-
-            @pl.when((done >= 0) & (done < SLOTS))
-            def _():
-                kernel_load(part, done, parity).start()
-
-            @pl.when(current == SLOTS)
+                    drained(
+                        sized(counts[part] // 2 * members, keeps(phase)), core_recv.at[part, chunk]
+                    )
+
+                load_start(part, chunk, slot)
+
+            def multiply(chunk, phase):
+                kernel_load(part, chunk, phase % 2).wait()
+                slip_wait(part, phase % 2)
+                product(part, chunk, phase % 2, phase)
+
+            def fetch(chunk, phase):
+                kernel_load(part, chunk, phase % 2).start()
+
+            at_chunk(at, phase, LAGS[part] + 1, load)
+            at_chunk(at, phase, LAGS[part] + 2, multiply)
+            at_chunk(at, phase, LAGS[part], fetch)
+
+            @pl.when(at - LAGS[part] - 2 == SLOTS)
             def _():
                 reduce_start(part)
 
-    def begin(pair, carry):
-        for parity in range(2):
-            chunk = 2 * pair + parity
+    def begin(group, carry):
+        for phase in range(PHASES):
+            chunk = group * PHASES + phase
 
             @pl.when(inner)
             def _():
-                pass_on(0, MIDDLE[0][1], chunk, parity, True)
+                for code, link, late in MIDDLE_SENDS:
+                    if late < 0:
+                        send(code, link, chunk, phase, True)
 
             @pl.when(outer)
             def _():
-                pass_on(0, CORNER[0][1], chunk, parity, False)
+                for code, link, late in CORNER_SENDS:
+                    if late < 0:
+                        send(code, link, chunk, phase, False)
 
         return carry
 
-    def travel(pair, carry):
-        for parity in range(2):
-            step(2 * pair + parity, parity)
+    def travel(group, carry):
+        for phase in range(PHASES):
+            step(group * PHASES + phase, phase)
         return carry
 
-    lax.fori_loop(0, AHEAD // 2, begin, 0)
-    lax.fori_loop(0, (SLOTS + 4 * LAG + 4) // 2, travel, 0)
-
-    kept = SLOTS // 2 * pair_keeps
+    lax.fori_loop(0, AHEAD // PHASES, begin, 0)
+    lax.fori_loop(0, pl.cdiv(SLOTS + LAGS[1] + 3, PHASES), travel, 0)
 
     @pl.when(inner)
     def _():
         drained(sized(3 * members, columns), links_send.at[0])
         drained(sized(3 * members, columns), links_send.at[1])
         drained(sized(3 * members, kept), links_send.at[2])
-        drained(sized(members, SLOTS // 2 * keeps(1)), links_send.at[3])
+        drained(sized(members, direct), links_send.at[3])
         drained(sized(members * rows // 2, columns), core_send)
 
     @pl.when(outer)
     def _():
         drained(sized(members, columns), links_send.at[0])
         drained(sized(3 * members, kept), links_send.at[2])
-        drained(sized(members, SLOTS // 2 * keeps(0)), links_send.at[3])
+        drained(sized(members, kept - direct), links_send.at[3])
         drained(shipped, links_send.at[4])
         drained(sized(members * rows // 2, kept), core_send)
 
-    span = out.shape[1] // 2
+    spans = [count * members for count in counts]
     for part in range(2):
         exchange(part).wait_recv()
-    for where in range(2):
-        out[:, pl.ds(where * span, span)] = total[where, rows_for(column)] + crossed[where]
 
     @pl.when(outer)
     def _():
         for part in range(2):
             for turned in range(2):
                 give_back(part, turned).wait_recv()
-        for where in range(2):
-            out[:, pl.ds(where * span, span)] += returned[0, where] + returned[1, where]
+
+    for low in range(2):
+
+        @pl.when(end == low)
+        def _():
+            for part in range(2):
+                first = (0, spans[0])[part] if low == 0 else (spans[1], 0)[part]
+                there = pl.ds(first, spans[part])
+                out[:, there] = total[part][rows_for(column), :] + crossed[part][...]
+
+                @pl.when(outer)
+                def _():
+                    out[:, there] += returned[part][0] + returned[part][1]
 
     for part in range(2):
         exchange(part).wait_send()
@@ -634,7 +677,8 @@
     targets, columns = kernel.shape
     members = slip.shape[0] * rows
     width = columns // SLOTS
-    away = SLOTS // 2 * (width // 8 * 3)
+    away = SLOTS // PHASES * (width // 8 * sum(SHIPS))
+    parts = (members // 2, members // 2)
     dma = pltpu.SemaphoreType.DMA
     return pl.pallas_call(
         functools.partial(grid_product, rows),
@@ -645,13 +689,13 @@
         in_specs=[pl.BlockSpec(memory_space=pl.ANY)] * 2,
         out_specs=(pl.BlockSpec(memory_space=pltpu.VMEM), pl.BlockSpec(memory_space=pl.ANY)),
         scratch_shapes=[
-            pltpu.VMEM((2, 2, members // 2, width), jnp.float32),
+            [pltpu.VMEM((2, part, width), jnp.float32) for part in parts],
             pltpu.VMEM((2, 2, targets, width), jnp.float32),
             pltpu.VMEM((targets, away), jnp.float32),
-            pltpu.VMEM((2, targets, members // 2), jnp.float32),
-            pltpu.VMEM((2, targets, members // 2), jnp.float32),
-            pltpu.VMEM((2, targets // 2, members // 2), jnp.float32),
-            pltpu.VMEM((2, 2, targets // 2, members // 2), jnp.float32),
+            [pltpu.VMEM((targets, part), jnp.float32) for part in parts],
+            [pltpu.VMEM((targets, part), jnp.float32) for part in parts],
+            [pltpu.VMEM((targets // 2, part), jnp.float32) for part in parts],
+            [pltpu.VMEM((2, targets // 2, part), jnp.float32) for part in parts],
             dma((5,)),
             dma((8, SLOTS)),
             dma,
@@ -664,7 +708,7 @@
             dma((2, 2)),
         ],
         compiler_params=pltpu.CompilerParams(
-            has_side_effects=True, vmem_limit_bytes=48 * 1024 * 1024
+            has_side_effects=True, vmem_limit_bytes=60 * 1024 * 1024
         ),
         cost_estimate=pl.CostEstimate(
             flops=6 * targets * members * columns,

time: 317 us -> 310 us (0.978)
  Pallas kernels: 309 us -> 304 us
    pallas_call x1, Pallas kernels: 309 us -> 304 us  [grid_traction(): pl.pallas_call(functools.partial(grid_product, rows), out_shape=(jax.Shap...]
where the time goes in v3:
time: 310 us
  Pallas kernels  304 us (98%)
    pallas_call x1, Pallas kernels, grid_traction(): pl.pallas_call(functools.partial(grid_product, rows), out_shape=(jax.Shap...  304 us

profile of v3, /device:TPU:0, one launch (start us, length us, event | category | flops | bytes accessed | tf_op | source)
XLA Modules:
  0.0 310.2 jit_solution(11417055074200969353)
XLA Ops:
  0.6 0.0 copy-start
  0.6 0.6 copy-done
  1.3 0.9 fusion.3
  2.2 1.0 fusion.4
  3.1 0.8 divide_negate_fusion
  3.9 0.0 copy-start.1
  3.9 0.0 copy-start.2
  3.9 304.0 %shard_map.95 = (f32[160,512]{1,0:T(8,128)}, f32[512,32768]{1,0:T(8,128)}) custom-call(f32[320,32768]{1,0:T(8,128)} %kernel_ref.1, f32[32,32768]{1,0:T(8,128)} %slip_ref.1), custom_call_target="tpu_custom_call" | custom-call | flops 32212254720 | bytes 268435456 | tf_op jit(solution)/shard_map/pallas_call | solution.py:683
  307.9 0.0 copy-done.1
  307.9 0.0 copy-done.2
  307.9 2.3 multiply_add_fusion
Async XLA Ops:
  0.6 0.7 copy-start
  3.9 304.0 %copy-start.1 = (f32[160,512]{1,0:T(8,128)S(1)}, f32[160,512]{1,0:T(8,128)}, u32[]{:S(2)}) copy-start(f32[160,512]{1,0:T(8,128)} %param.12) | copy-start | bytes 983044
  3.9 304.0 %copy-start.2 = (f32[160,512]{1,0:T(8,128)S(1)}, f32[160,512]{1,0:T(8,128)}, u32[]{:S(2)}) copy-start(f32[160,512]{1,0:T(8,128)} %param.11) | copy-start | bytes 983044
